TPU v7x, 32 devices: a whole 2x2x4 slice. The times are simulated.
32 devices in a mesh: dp: 8 (over z, y), tensor: 4 (over x, core).
Axes of the slice: x: 2, y: 2, z: 4, core: 2. Of those that a mesh axis runs over, the one named last changes fastest.
Arguments:
- queries: bfloat16 [16, 512, 3072], P('dp', None, 'tensor'), may hold values from -110 to 110
- draft_key_value: bfloat16 [16, 2, 512, 512], P('dp', None, None, 'tensor'), may hold values from -4.5 to 4.5
- cache_kv: bfloat16 [16, 2, 1792, 512], P('dp', None, None, 'tensor'), may hold values from -6 to 6
- out_weight: bfloat16 [3072, 6144], P('tensor'), may hold values from -0.109375 to 0.109375
- tree_sizes: int32 [16], replicated, may hold values from 16 to 512
- parents: int32 [16, 512], replicated, may hold values from 0 to 511, as said below
- cache_lens: int32 [16], replicated, may hold values from 448 to 1792
- block_moves: int32 [8, 2], replicated, may hold values from 0 to 7, as said below
Outputs:
- own_out: bfloat16 [8192, 6144], P(('dp', 'tensor'))
- moved_out: bfloat16 [1024, 6144], P(('dp', 'tensor'))
Inputs may be any that keep to these rules, and one draw needn't show every extreme that they name: parents[r, 0] = 0 and parents[r, i] < i for every i >= 1. `block_moves`: row d is (destination, slot). The destination is d itself (nothing moves, slot 0) or differs from d in exactly one bit. No device is the destination of two others, and a device that gives a block away takes none. A moved slot (r mod 2) * 4 + k names a block with k * 128 < tree_sizes[r] of one of d's requests r.
All inputs are finite; a program needn't handle non-finite values.
Results may differ from a plain program's by a relative error of at most 0.01.
Values may be sent and summed in bfloat16 or wider, within the bound.
A program may use at most 128 MiB of HBM per device.

v0:
```python
import functools
import math

import jax
import jax.numpy as jnp
from jax import lax
from jax.experimental import pallas as pl
from jax.experimental.pallas import tpu as pltpu
from jax.sharding import PartitionSpec as P


HEAD_SIZE = 128
BLK = 128
SCALE = HEAD_SIZE**-0.5 * math.log2(math.e)
LOW = -1e30
CHUNK = 512
TILES = 3
PIECES = 2


def swapped(array, axis, bit):
    return lax.ppermute(array, axis, [(i, i ^ bit) for i in range(lax.axis_size(axis))])


def reach_kernel(ids_ref, parent_ref, bias_ref, reach_ref):
    requests, nodes, _ = reach_ref.shape
    blocks = nodes // BLK
    spots = [(r, b) for r in range(requests) for b in range(blocks)]
    row = lax.broadcasted_iota(jnp.int32, (BLK, BLK), 0)
    column = lax.broadcasted_iota(jnp.int32, (BLK, BLK), 1)
    ups, insides = {}, {}
    for r, b in spots:
        up = parent_ref[0, r : r + 1, b * BLK : (b + 1) * BLK]
        ups[r, b] = jnp.broadcast_to(up, (BLK, BLK)).T
        linked = (row == column) | (ups[r, b] == column + b * BLK)
        insides[r, b] = jnp.where(linked, 1.0, 0.0).astype(jnp.bfloat16)
    for _ in range((BLK - 1).bit_length()):
        for at in spots:
            squared = jnp.dot(insides[at], insides[at], preferred_element_type=jnp.float32)
            insides[at] = jnp.where(squared > 0.5, 1.0, 0.0).astype(jnp.bfloat16)
    for b in range(blocks):
        for r in range(requests):
            rows = pl.ds(b * BLK, BLK)
            for k in range(blocks):
                if k >= b:
                    part = insides[r, b] if k == b else jnp.zeros((BLK, BLK), jnp.bfloat16)
                    reach_ref[r, rows, k * BLK : (k + 1) * BLK] = part
            if b:
                steps = [ups[r, b] == column + k * BLK for k in range(b)]
                step = jnp.concatenate(
                    [jnp.where(one, 1.0, 0.0).astype(jnp.bfloat16) for one in steps], axis=1
                )
                outer = jnp.dot(
                    step, reach_ref[r, : b * BLK, : b * BLK], preferred_element_type=jnp.float32
                ).astype(jnp.bfloat16)
                reach_ref[r, rows, : b * BLK] = jnp.dot(
                    insides[r, b], outer, preferred_element_type=jnp.float32
                ).astype(jnp.bfloat16)
            bias_ref[r, rows, :] = jnp.where(
                reach_ref[r, rows, :].astype(jnp.float32) > 0.5, 0.0, LOW
            )


def reach_bias(ids, parents, requests):
    nodes = parents.shape[1]
    return pl.pallas_call(
        reach_kernel,
        out_shape=jax.ShapeDtypeStruct((requests, nodes, nodes), jnp.float32),
        grid_spec=pltpu.PrefetchScalarGridSpec(
            num_scalar_prefetch=1,
            grid=(1,),
            in_specs=[pl.BlockSpec((1, requests, nodes), lambda s, m: (m[0], 0, 0))],
            out_specs=pl.BlockSpec((requests, nodes, nodes), lambda s, m: (0, 0, 0)),
            scratch_shapes=[pltpu.VMEM((requests, nodes, nodes), jnp.bfloat16)],
        ),
        cost_estimate=pl.CostEstimate(
            flops=10**9, bytes_accessed=4 * requests * nodes * nodes, transcendentals=0
        ),
        name="reach",
    )(ids, parents.reshape(-1, requests, nodes))


def attend_kernel(
    slot_of,
    given,
    ids_ref,
    sizes_ref,
    lengths_ref,
    moves_ref,
    q_ref,
    draft_ref,
    cache_ref,
    bias_ref,
    after_ref,
    out_ref,
    stack_ref,
    top_ref,
    total_ref,
):
    blocks = draft_ref.shape[2] // BLK
    step = pl.program_id(0)
    slot = slot_of(step, ids_ref, moves_ref)
    mine = ids_ref[0]
    request, block = slot // blocks, slot % blocks
    per_device = sizes_ref.shape[0] // moves_ref.shape[0]
    size = sizes_ref[mine * per_device + request]
    length = lengths_ref[mine * per_device + request]
    moved = (moves_ref[mine, 0] != mine) & (moves_ref[mine, 1] == slot)
    wanted = moved == (step >= given)
    active = (wanted & (block * BLK < size)).astype(jnp.int32)
    heads = q_ref.shape[2] // HEAD_SIZE
    rows = heads * BLK
    tile = rows // TILES
    slots = cache_ref.shape[2]
    nodes = draft_ref.shape[2]

    def scores(at, keys):
        return (
            lax.dot_general(
                stack_ref[pl.ds(at, tile), :],
                keys,
                (((1,), (1,)), ((), ())),
                preferred_element_type=jnp.float32,
            )
            * SCALE
        )

    def widened(values):
        return jnp.concatenate([values, jnp.ones(values.shape, values.dtype)], axis=1)

    def tree(width):
        keys = draft_ref[0, 0, :width, :]
        values = widened(draft_ref[0, 1, :width, :])
        bias = bias_ref[0, :, :width]
        bias = jnp.concatenate([bias] * (tile // BLK), axis=0)
        for part in range(TILES):
            at = part * tile
            s = scores(at, keys) + bias
            top = jnp.max(s, axis=1, keepdims=True)
            p = jnp.exp2(s - top).astype(jnp.bfloat16)
            top_ref[pl.ds(at, tile), :] = jnp.broadcast_to(top, (tile, HEAD_SIZE))
            total_ref[pl.ds(at, tile), :] = jnp.dot(p, values, preferred_element_type=jnp.float32)

    @pl.when(active == 0)
    def _():
        out_ref[...] = jnp.zeros_like(out_ref)

    @pl.when(active != 0)
    def _():
        for head in range(heads):
            stack_ref[head * BLK : (head + 1) * BLK, :] = q_ref[
                0, :, head * HEAD_SIZE : (head + 1) * HEAD_SIZE
            ]
        half = nodes // 2

        @pl.when((block + 1) * BLK <= half)
        def _():
            tree(half)

        @pl.when((block + 1) * BLK > half)
        def _():
            tree(nodes)

        def chunk(index, _):
            first = index * CHUNK
            start = pl.multiple_of(jnp.minimum(first, slots - CHUNK), BLK)
            keys = cache_ref[0, 0, pl.ds(start, CHUNK), :]
            values = widened(cache_ref[0, 1, pl.ds(start, CHUNK), :])
            position = lax.broadcasted_iota(jnp.int32, (1, CHUNK), 1) + start
            bias = jnp.where((position >= first) & (position < length), 0.0, LOW)
            for part in range(TILES):
                at = part * tile
                s = scores(at, keys) + bias
                old = top_ref[pl.ds(at, tile), :][:, :1]
                top = jnp.maximum(old, jnp.max(s, axis=1, keepdims=True))
                p = jnp.exp2(s - top).astype(jnp.bfloat16)
                shrink = jnp.exp2(old - top)
                top_ref[pl.ds(at, tile), :] = jnp.broadcast_to(top, (tile, HEAD_SIZE))
                total_ref[pl.ds(at, tile), :] = total_ref[pl.ds(at, tile), :] * shrink + jnp.dot(
                    p, values, preferred_element_type=jnp.float32
                )
            return 0

        lax.fori_loop(0, (length + CHUNK - 1) // CHUNK, chunk, 0)
        live = block * BLK + lax.broadcasted_iota(jnp.int32, (BLK, HEAD_SIZE), 0) < size
        for head in range(heads):
            at = head * BLK
            result = total_ref[at : at + BLK, :HEAD_SIZE] / total_ref[at : at + BLK, HEAD_SIZE:]
            out_ref[:, head * HEAD_SIZE : (head + 1) * HEAD_SIZE] = jnp.where(
                live, result, 0.0
            ).astype(out_ref.dtype)


def attend(scalars, slot_of, steps, given, queries, draft, cache, bias, after):
    width = queries.shape[2]
    nodes = draft.shape[2]
    slots = cache.shape[2]
    blocks = nodes // BLK
    rows = width // HEAD_SIZE * BLK

    def request(s, ids, sizes, lengths, moves):
        return slot_of(s, ids, moves) // blocks, 0, 0, 0

    def rows_at(s, ids, sizes, lengths, moves):
        slot = slot_of(s, ids, moves)
        return slot // blocks, slot % blocks, 0

    grid_spec = pltpu.PrefetchScalarGridSpec(
        num_scalar_prefetch=4,
        grid=(steps,),
        in_specs=[
            pl.BlockSpec((1, BLK, width), rows_at),
            pl.BlockSpec((1, 2, nodes, HEAD_SIZE), request),
            pl.BlockSpec((1, 2, slots, HEAD_SIZE), request),
            pl.BlockSpec((1, BLK, nodes), rows_at),
            pl.BlockSpec(memory_space=pl.ANY),
        ],
        out_specs=pl.BlockSpec((BLK, width), lambda s, *_: (s, 0)),
        scratch_shapes=[
            pltpu.VMEM((rows, HEAD_SIZE), jnp.bfloat16),
            pltpu.VMEM((rows, HEAD_SIZE), jnp.float32),
            pltpu.VMEM((rows, 2 * HEAD_SIZE), jnp.float32),
        ],
    )
    return pl.pallas_call(
        functools.partial(attend_kernel, slot_of, given),
        out_shape=jax.ShapeDtypeStruct((steps * BLK, width), queries.dtype),
        grid_spec=grid_spec,
        cost_estimate=pl.CostEstimate(
            flops=steps * rows * (nodes + slots) * HEAD_SIZE * 4,
            bytes_accessed=4 * (nodes + slots) * HEAD_SIZE * 2 + steps * BLK * width * 4,
            transcendentals=steps * rows * (nodes + slots),
        ),
    )(*scalars, queries, draft, cache, bias, after)


def local(
    queries, draft_key_value, cache_kv, out_weight, tree_sizes, parents, cache_lens, block_moves
):
    requests, nodes, width = queries.shape
    blocks = nodes // BLK
    dp_count = lax.axis_size("dp")
    mine = lax.axis_index("dp")
    tensor_count = lax.axis_size("tensor")
    spot = lax.axis_index("tensor")
    pairs = tensor_count // 2
    high, low = spot // 2, spot % 2
    ids = jnp.stack([mine, high, low]).astype(jnp.int32)
    scalars = (ids, tree_sizes, cache_lens, block_moves)
    sibling_weight = swapped(out_weight, "tensor", 1)
    bias = reach_bias(ids, parents, requests)
    per_pair = requests * blocks // pairs
    per_core = per_pair // 2

    def cores_share(rows):
        ours = lax.dynamic_index_in_dim(rows, low, 0, keepdims=False)
        theirs = lax.dynamic_index_in_dim(rows, 1 - low, 0, keepdims=False)
        return ours, swapped(theirs, "tensor", 1)

    def kept_rows(hop, first, count, giving, after):
        def slot_of(s, ids, moves):
            part = (ids[1] + hop) % pairs
            slot = part * per_pair + (s // count) * per_core + first + s % count
            return jnp.where(s >= 2 * count, moves[ids[0], 1], slot)

        rows = attend(
            scalars, slot_of, 2 * count + giving, 2 * count, queries, draft_key_value,
            cache_kv, bias, after,
        )
        split = 2 * count * BLK
        return cores_share(rows[:split].reshape(2, count * BLK, width)), rows[split:]

    def product(rows, piece, pieces):
        columns = out_weight.shape[1] // pieces
        at = slice(piece * columns, (piece + 1) * columns)
        ours, theirs = rows
        total = jnp.dot(ours, out_weight[:, at], preferred_element_type=jnp.float32)
        return total + jnp.dot(theirs, sibling_weight[:, at], preferred_element_type=jnp.float32)

    def onward(part, hop):
        ring = [
            (2 * h + l, 2 * ((h + hop) % pairs) + l) for h in range(pairs) for l in range(2)
        ]
        return lax.ppermute(part, "tensor", ring)

    coming = {}
    after = bias
    for hop in range(1, pairs):
        for sub in range(per_core):
            giving = int((hop, sub) == (1, per_core - 1))
            rows, given = kept_rows(hop, sub, 1, giving, after)
            for piece in range(PIECES):
                part = product(rows, piece, PIECES).astype(jnp.bfloat16)
                coming.setdefault((sub, piece), []).append(onward(part, hop))
            after = part
            if giving:
                target = block_moves[:, 0]
                numbers = jnp.arange(dp_count, dtype=jnp.int32)
                arrives = (target == mine) & (target != numbers)
                present = jnp.any(arrives)
                bits = jnp.bitwise_xor(jnp.sum(jnp.where(arrives, numbers, 0)), mine)
                arrived = jnp.zeros_like(given)
                for bit in range(dp_count.bit_length() - 1):
                    fresh = swapped(given, "dp", 1 << bit)
                    arrived = jnp.where(present & (bits == 1 << bit), fresh, arrived)
                arrived = arrived.reshape(pairs, 2, -1, width)
    ours, _ = kept_rows(0, 0, per_core, 0, after)

    def new_rows(hop):
        part = lax.dynamic_index_in_dim(arrived, (high + hop) % pairs, 0, keepdims=False)
        return cores_share(part)

    new_coming = [
        onward(product(new_rows(hop), 0, 1).astype(jnp.bfloat16), hop)
        for hop in range(1, pairs)
    ]

    def total_of(rows, piece, pieces, parts):
        total = lax.optimization_barrier(product(rows, piece, pieces))
        for part in parts:
            total = total + part.astype(jnp.float32)
        return total.astype(jnp.bfloat16)

    done = []
    for sub in range(per_core):
        rows = tuple(one[sub * BLK : (sub + 1) * BLK] for one in ours)
        pieces = [total_of(rows, piece, PIECES, coming[sub, piece]) for piece in range(PIECES)]
        done.append(jnp.concatenate(pieces, axis=1))
    own_out = jnp.concatenate(done, axis=0)
    moved_out = total_of(new_rows(0), 0, 1, new_coming)
    return own_out, moved_out


def solution(mesh):
    in_specs = (
        P("dp", None, "tensor"),
        P("dp", None, None, "tensor"),
        P("dp", None, None, "tensor"),
        P("tensor", None),
        P(),
        P(),
        P(),
        P(),
    )
    out_specs = (P(("dp", "tensor"), None), P(("dp", "tensor"), None))

    def build(queries, *rest):
        step = jax.shard_map(
            local, mesh=mesh, in_specs=in_specs, out_specs=out_specs, check_vma=False
        )
        return step(queries, *rest)

    return build
```

profile of v0, /device:TPU:22, one launch (start us, length us, event | category | flops | bytes accessed | tf_op | source)
XLA Modules:
  0.0 173.6 jit_solution(14441774976132017234)
XLA Ops:
  0.6 0.1 collective-permute-start.1
  0.7 1.3 copy.12.moves_ref
  2.1 1.4 reshape.29.parent_ref
  3.5 0.7 pad_add_fusion.ids_ref
  4.1 4.9 %reach.1.bias_ref.after_ref = f32[2,512,512]{2,1,0:T(8,128)} custom-call(s32[3]{0:T(128)} %pad_add_fusion.ids_ref, s32[8,2,512]{2,1,0:T(2,128)} %reshape.29.parent_ref), custom_call_target="tpu_custom_call" | custom-call | flops 1000000000 | bytes 2097152 | tf_op jit(solution)/shard_map/reach/pallas_call | solution.py:66
  9.0 13.8 %shard_map.95 = bf16[256,768]{1,0:T(8,128)(2,1)} custom-call(s32[3]{0:T(128)} %pad_add_fusion.ids_ref, s32[16]{0:T(128)} %sizes_ref.5, s32[16]{0:T(128)} %lengths_ref.5, s32[8,2]{1,0:T(8,128)} %copy.12.moves_ref, bf16[2,512,768]{2,1,0:T(8,128)(2,1)} %q_ref.5, bf16[2,2,512,128]{3,2,1,0:T(8,128)(2,1)} %draft_ref.5, bf16[2,2,1792,128]{3,2,1,0:T(8,128)(2,1)} %cache_ref.5, ...), custom_call_target="tpu_custom_call" | custom-call | flops 1811939328 | bytes 3145728 | tf_op jit(solution)/shard_map/pallas_call | solution.py:225
  22.9 1.7 dynamic-slice_bitcast_fusion.4
  24.6 0.5 collective-permute-start
  25.0 3.2 %fusion.17 = f32[128,3072]{1,0:T(8,128)S(1)} fusion(bf16[768,6144]{1,0:T(8,128)(2,1)} %param.11, bf16[2,128,768]{2,1,0:T(8,128)(2,1)} %bitcast.57, s32[]{:T(128)S(6)} %select_n.77), kind=kOutput, calls=%fused_computation.28 | convolution fusion | flops 603979776 | bytes 6488068 | tf_op jit(solution)/shard_map/dot_general | solution.py:277
  28.3 0.0 copy-start.3
  28.3 3.1 %fusion.27 = f32[128,3072]{1,0:T(8,128)S(1)} fusion(bf16[768,6144]{1,0:T(8,128)(2,1)} %param.11, bf16[2,128,768]{2,1,0:T(8,128)(2,1)S(1)} %bitcast.58, s32[]{:T(128)S(6)} %select_n.77), kind=kOutput, calls=%fused_computation.38 | convolution fusion | flops 603979776 | bytes 6488068 | tf_op jit(solution)/shard_map/dot_general | solution.py:277
  31.4 0.6 select_reduce_fusion
  32.7 0.6 reduce_or.9
  35.3 0.0 collective-permute-done
  35.3 0.0 collective-permute-done.1
  35.3 4.1 %fusion.1.after_ref = bf16[128,3072]{1,0:T(8,128)(2,1)} fusion(f32[128,3072]{1,0:T(8,128)S(1)} %fusion.27, bf16[128,768]{1,0:T(8,128)(2,1)} %collective-permute-done, bf16[768,6144]{1,0:T(8,128)(2,1)} %collective-permute-done.1), kind=kOutput, calls=%fused_computation.11 | convolution fusion | flops 604766208 | bytes 7274496 | tf_op jit(solution)/shard_map/dot_general | solution.py:278
  39.5 18.1 %shard_map.96 = bf16[384,768]{1,0:T(8,128)(2,1)} custom-call(s32[3]{0:T(128)} %pad_add_fusion.ids_ref, s32[16]{0:T(128)} %sizes_ref.5, s32[16]{0:T(128)} %lengths_ref.5, s32[8,2]{1,0:T(8,128)} %copy.12.moves_ref, bf16[2,512,768]{2,1,0:T(8,128)(2,1)} %q_ref.5, bf16[2,2,512,128]{3,2,1,0:T(8,128)(2,1)} %draft_ref.5, bf16[2,2,1792,128]{3,2,1,0:T(8,128)(2,1)} %cache_ref.5, ...), custom_call_target="tpu_custom_call" | custom-call | flops 2717908992 | bytes 3538944 | tf_op jit(solution)/shard_map/pallas_call | solution.py:225
  57.6 0.9 slice.69
  58.5 1.0 slice.65
  59.6 0.1 collective-permute-start.10
  59.6 0.1 collective-permute-start.9
  59.7 0.1 collective-permute-start.8
  59.8 0.1 collective-permute-start.5
  59.9 3.2 %fusion.13 = f32[128,3072]{1,0:T(8,128)S(1)} fusion(bf16[768,6144]{1,0:T(8,128)(2,1)} %param.11, bf16[2,128,768]{2,1,0:T(8,128)(2,1)S(1)} %bitcast.60, s32[]{:T(128)S(6)} %select_n.77), kind=kOutput, calls=%fused_computation.24 | convolution fusion | flops 603979776 | bytes 6488068 | tf_op jit(solution)/shard_map/dot_general | solution.py:277
  63.1 0.1 collective-permute-start.2
  63.2 4.1 %fusion.3 = bf16[128,3072]{1,0:T(8,128)(2,1)} fusion(f32[128,3072]{1,0:T(8,128)S(1)} %fusion.17, bf16[128,768]{1,0:T(8,128)(2,1)} %collective-permute-done, bf16[768,6144]{1,0:T(8,128)(2,1)} %collective-permute-done.1), kind=kOutput, calls=%fused_computation.13 | convolution fusion | flops 604766208 | bytes 7274496 | tf_op jit(solution)/shard_map/dot_general | solution.py:278
  67.3 3.1 %fusion.25 = f32[128,3072]{1,0:T(8,128)S(1)} fusion(bf16[768,6144]{1,0:T(8,128)(2,1)} %param.11, bf16[2,128,768]{2,1,0:T(8,128)(2,1)S(1)} %bitcast.61, s32[]{:T(128)S(6)} %select_n.77), kind=kOutput, calls=%fused_computation.36 | convolution fusion | flops 603979776 | bytes 6488068 | tf_op jit(solution)/shard_map/dot_general | solution.py:277
  70.4 0.0 collective-permute-done.2
  70.4 2.0 %collective-permute-start.4 = (bf16[128,3072]{1,0:T(8,128)(2,1)}, bf16[128,3072]{1,0:T(8,128)(2,1)S(1)}, u32[]{:S(2)}, u32[]{:S(2)}) collective-permute-start(bf16[128,3072]{1,0:T(8,128)(2,1)} %fusion.3), channel_id=1, source_target_pairs={{0,2},{1,3},{2,0},{3,1},{4,6},{5,7},{6,4},{7,5},{8,10},{9,11},{10,... | collective-permute-start | bytes 2359304 | tf_op jit(solution)/shard_map/ppermute | solution.py:284
  72.5 4.1 %fusion.2.after_ref = bf16[128,3072]{1,0:T(8,128)(2,1)} fusion(f32[128,3072]{1,0:T(8,128)S(1)} %fusion.25, bf16[128,768]{1,0:T(8,128)(2,1)S(1)} %collective-permute-done.2, bf16[768,6144]{1,0:T(8,128)(2,1)} %collective-permute-done.1), kind=kOutput, calls=%fused_computation.12 | convolution fusion | flops 604766208 | bytes 7274496 | tf_op jit(solution)/shard_map/dot_general | solution.py:278
  76.6 16.5 %shard_map.97 = bf16[512,768]{1,0:T(8,128)(2,1)} custom-call(s32[3]{0:T(128)} %pad_add_fusion.ids_ref, s32[16]{0:T(128)} %sizes_ref.5, s32[16]{0:T(128)} %lengths_ref.5, s32[8,2]{1,0:T(8,128)} %copy.12.moves_ref, bf16[2,512,768]{2,1,0:T(8,128)(2,1)} %q_ref.5, bf16[2,2,512,128]{3,2,1,0:T(8,128)(2,1)} %draft_ref.5, bf16[2,2,1792,128]{3,2,1,0:T(8,128)(2,1)} %cache_ref.5, ...), custom_call_target="tpu_custom_call" | custom-call | flops 3623878656 | bytes 3932160 | tf_op jit(solution)/shard_map/pallas_call | solution.py:225
  93.1 3.4 %fusion.21 = f32[128,3072]{1,0:T(8,128)S(1)} fusion(bf16[768,6144]{1,0:T(8,128)(2,1)} %param.11, bf16[2,256,768]{2,1,0:T(8,128)(2,1)} %bitcast.62, s32[]{:T(128)S(6)} %select_n.77, s32[]{:T(128)S(6)} %add.125), kind=kOutput, calls=%fused_computation.32 | convolution fusion | flops 603979776 | bytes 6488072 | tf_op jit(solution)/shard_map/dot_general | solution.py:277
  96.5 0.0 slice-start.2
  96.5 3.9 %fusion.15 = f32[128,3072]{1,0:T(8,128)S(1)} fusion(bf16[768,6144]{1,0:T(8,128)(2,1)} %param.11, bf16[2,256,768]{2,1,0:T(8,128)(2,1)S(1)} %bitcast.63, s32[]{:T(128)S(6)} %select_n.77, s32[]{:T(128)S(6)} %add.125), kind=kOutput, calls=%fused_computation.26 | convolution fusion | flops 603979776 | bytes 6488072 | tf_op jit(solution)/shard_map/dot_general | solution.py:277
  100.4 3.1 %fusion.23 = f32[128,3072]{1,0:T(8,128)S(1)} fusion(bf16[768,6144]{1,0:T(8,128)(2,1)} %param.11, bf16[2,256,768]{2,1,0:T(8,128)(2,1)S(1)} %bitcast.64, s32[]{:T(128)S(6)} %select_n.77), kind=kOutput, calls=%fused_computation.34 | convolution fusion | flops 603979776 | bytes 6488068 | tf_op jit(solution)/shard_map/dot_general | solution.py:277
  103.6 0.8 fusion.19
  104.4 0.0 collective-permute-done.10
  104.4 0.3 copy-done.2
  104.8 8.7 %collective-permute-start.7 = (bf16[128,3072]{1,0:T(8,128)(2,1)S(1)}, bf16[128,3072]{1,0:T(8,128)(2,1)S(1)}, u32[]{:S(2)}, u32[]{:S(2)}) collective-permute-start(bf16[128,3072]{1,0:T(8,128)(2,1)S(1)} %copy-done.2), channel_id=1, source_target_pairs={{0,2},{1,3},{2,0},{3,1},{4,6},{5,7},{6,4},{7,5},{8,10},{9,11},{10,... | collective-permute-start | bytes 2359304 | tf_op jit(solution)/shard_map/ppermute | solution.py:284
  113.4 0.0 collective-permute-done.9
  113.4 0.0 collective-permute-done.8
  113.5 0.2 collective-permute-start.11
  113.8 3.1 %fusion.4 = bf16[128,3072]{1,0:T(8,128)(2,1)S(1)} fusion(f32[128,3072]{1,0:T(8,128)S(1)} %fusion.13, bf16[128,768]{1,0:T(8,128)(2,1)S(1)} %collective-permute-done.2, bf16[768,6144]{1,0:T(8,128)(2,1)} %collective-permute-done.1), kind=kOutput, calls=%fused_computation.14 | convolution fusion | flops 604766208 | bytes 7274496 | tf_op jit(solution)/shard_map/dot_general | solution.py:278
  116.9 0.4 collective-permute-start.12
  117.3 0.0 collective-permute-start.6
  117.4 5.4 %fusion.55 = f32[32,6144]{1,0:T(8,128)S(1)} fusion(bf16[32,768]{1,0:T(8,128)(2,1)S(1)} %collective-permute-done.11, bf16[768,6144]{1,0:T(8,128)(2,1)} %collective-permute-done.1), kind=kOutput, calls=%fused_computation.82 | convolution fusion | flops 301989888 | bytes 10272768 | tf_op jit(solution)/shard_map/dot_general | solution.py:278
  122.8 1.7 convolution_add_fusion.1
  124.5 0.0 collective-permute-done.12
  124.6 0.2 collective-permute-start.3
  124.8 5.4 %fusion.56 = f32[32,6144]{1,0:T(8,128)S(1)} fusion(bf16[32,768]{1,0:T(8,128)(2,1)S(1)} %collective-permute-done.12, bf16[768,6144]{1,0:T(8,128)(2,1)} %collective-permute-done.1), kind=kOutput, calls=%fused_computation.83 | convolution fusion | flops 301989888 | bytes 10272768 | tf_op jit(solution)/shard_map/dot_general | solution.py:278
  130.2 1.7 fusion
  131.9 0.0 collective-permute-done.3
  132.0 1.9 %collective-permute-start.13 = (bf16[32,6144]{1,0:T(8,128)(2,1)S(1)}, bf16[32,6144]{1,0:T(8,128)(2,1)S(1)}, u32[]{:S(2)}, u32[]{:S(2)}) collective-permute-start(bf16[32,6144]{1,0:T(8,128)(2,1)S(1)} %fusion), channel_id=1, source_target_pairs={{0,2},{1,3},{2,0},{3,1},{4,6},{5,7},{6,4},{7,5},{8,10},{9,11},{10,... | collective-permute-start | bytes 1179656 | tf_op jit(solution)/shard_map/ppermute | solution.py:284
  133.9 3.2 %convolution_add_fusion.2 = f32[128,3072]{1,0:T(8,128)S(1)} fusion(f32[128,3072]{1,0:T(8,128)S(1)} %fusion.21, bf16[768,6144]{1,0:T(8,128)(2,1)} %collective-permute-done.1, bf16[256,768]{1,0:T(8,128)(2,1)S(1)} %collective-permute-done.3), kind=kOutput, calls=%fused_computation.3 | convolution fusion | flops 604372992 | bytes 8060928 | tf_op jit(solution)/shard_map/dot_general | solution.py:278
  137.1 3.2 %convolution_add_fusion.4 = f32[128,3072]{1,0:T(8,128)S(1)} fusion(f32[128,3072]{1,0:T(8,128)S(1)} %fusion.15, bf16[768,6144]{1,0:T(8,128)(2,1)} %collective-permute-done.1, bf16[256,768]{1,0:T(8,128)(2,1)S(1)} %collective-permute-done.3), kind=kOutput, calls=%fused_computation.5 | convolution fusion | flops 604372992 | bytes 8060928 | tf_op jit(solution)/shard_map/dot_general | solution.py:278
  140.3 3.2 %convolution_add_fusion.5 = f32[128,3072]{1,0:T(8,128)S(1)} fusion(f32[128,3072]{1,0:T(8,128)S(1)} %fusion.23, bf16[768,6144]{1,0:T(8,128)(2,1)} %collective-permute-done.1, bf16[256,768]{1,0:T(8,128)(2,1)S(1)} %collective-permute-done.3), kind=kOutput, calls=%fused_computation.6 | convolution fusion | flops 604372992 | bytes 8060928 | tf_op jit(solution)/shard_map/dot_general | solution.py:278
  143.5 3.5 %convolution_add_fusion.7 = f32[128,3072]{1,0:T(8,128)S(1)} fusion(f32[128,3072]{1,0:T(8,128)S(1)} %fusion.19, bf16[768,6144]{1,0:T(8,128)(2,1)} %collective-permute-done.1, bf16[256,768]{1,0:T(8,128)(2,1)S(1)} %collective-permute-done.3), kind=kOutput, calls=%fused_computation.8 | convolution fusion | flops 604372992 | bytes 8060928 | tf_op jit(solution)/shard_map/dot_general | solution.py:278
  147.0 9.9 %collective-permute-done.13 = bf16[32,6144]{1,0:T(8,128)(2,1)S(1)} collective-permute-done((bf16[32,6144]{1,0:T(8,128)(2,1)S(1)}, bf16[32,6144]{1,0:T(8,128)(2,1)S(1)}, u32[]{:S(2)}, u32[]{:S(2)}) %collective-permute-start.13) | collective-permute-done | bytes 393248 | tf_op jit(solution)/shard_map/ppermute | solution.py:284
  156.9 0.8 add_convert_fusion.4
  157.7 1.3 add_convert_fusion.2
  159.0 0.2 add_convert_fusion.3
  159.2 0.2 add_convert_fusion
  159.4 0.2 add_convert_fusion.1
  159.6 14.0 %maximum_maximum_fusion = bf16[256,6144]{1,0:T(8,128)(2,1)} fusion(bf16[128,3072]{1,0:T(8,128)(2,1)S(1)} %add_convert_fusion, bf16[128,3072]{1,0:T(8,128)(2,1)S(1)} %add_convert_fusion.1, bf16[128,3072]{1,0:T(8,128)(2,1)S(1)} %add_convert_fusion.2, bf16[128,3072]{1,0:T(8,128)(2,1)S(1)} %add_convert_fusion.3), kind=kLoop, calls=%fused_computation.15 | loop fusion | flops 12582912 | bytes 6291456 | tf_op jit(solution)/shard_map/concatenate | solution.py:329
  (21 shorter events, 0.2 us)
Async XLA Ops:
  0.6 34.7 %collective-permute-start.1 = (bf16[768,6144]{1,0:T(8,128)(2,1)}, bf16[768,6144]{1,0:T(8,128)(2,1)}, u32[]{:S(2)}, u32[]{:S(2)}) collective-permute-start(bf16[768,6144]{1,0:T(8,128)(2,1)} %param.11), channel_id=1, source_target_pairs={{0,1},{1,0},{2,3},{3,2},{4,5},{5,4},{6,7},{7,6},{8,9},{9,8},{10,11... | collective-permute-start | bytes 28311560 | tf_op jit(solution)/shard_map/ppermute | solution.py:22
  22.9 5.4 %copy-start = (bf16[256,768]{1,0:T(8,128)(2,1)S(1)}, bf16[256,768]{1,0:T(8,128)(2,1)}, u32[]{:S(2)}) copy-start(bf16[256,768]{1,0:T(8,128)(2,1)} %shard_map.95) | copy-start | bytes 1179652
  24.6 10.8 %collective-permute-start = (bf16[128,768]{1,0:T(8,128)(2,1)}, bf16[128,768]{1,0:T(8,128)(2,1)}, u32[]{:S(2)}, u32[]{:S(2)}) collective-permute-start(bf16[128,768]{1,0:T(8,128)(2,1)} %dynamic-slice_bitcast_fusion.4), channel_id=1, source_target_pairs={{0,1},{1,0},{2,3},{3,2},{4,5},{5,4},{6,7},{7,6},{8,9},{9,8},{10,11... | collective-permute-start | bytes 589832 | tf_op jit(solution)/shard_map/ppermute | solution.py:22
  28.3 3.1 %copy-start.3 = (s32[8,2]{0,1:T(2,128)S(1)}, s32[8,2]{0,1:T(2,128)}, u32[]{:S(2)}) copy-start(s32[8,2]{0,1:T(2,128)} %param.15) | copy-start | bytes 196
  59.6 44.9 %collective-permute-start.10 = (bf16[128,768]{1,0:T(8,128)(2,1)S(1)}, bf16[128,768]{1,0:T(8,128)(2,1)}, u32[]{:S(2)}, u32[]{:S(2)}) collective-permute-start(bf16[128,768]{1,0:T(8,128)(2,1)S(1)} %slice.69), channel_id=1, source_target_pairs={{0,4},{4,0},{8,12},{12,8},{16,20},{20,16},{24,28},{28,24},{1,5},{5... | collective-permute-start | bytes 589832 | tf_op jit(solution)/shard_map/ppermute | solution.py:22
  59.6 53.8 %collective-permute-start.9 = (bf16[128,768]{1,0:T(8,128)(2,1)S(1)}, bf16[128,768]{1,0:T(8,128)(2,1)}, u32[]{:S(2)}, u32[]{:S(2)}) collective-permute-start(bf16[128,768]{1,0:T(8,128)(2,1)S(1)} %slice.69), channel_id=1, source_target_pairs={{0,8},{4,12},{8,0},{12,4},{16,24},{20,28},{24,16},{28,20},{1,9},{5... | collective-permute-start | bytes 589832 | tf_op jit(solution)/shard_map/ppermute | solution.py:22
  59.7 53.7 %collective-permute-start.8 = (bf16[128,768]{1,0:T(8,128)(2,1)S(1)}, bf16[128,768]{1,0:T(8,128)(2,1)}, u32[]{:S(2)}, u32[]{:S(2)}) collective-permute-start(bf16[128,768]{1,0:T(8,128)(2,1)S(1)} %slice.69), channel_id=1, source_target_pairs={{0,16},{4,20},{8,24},{12,28},{16,0},{20,4},{24,8},{28,12},{1,17},{... | collective-permute-start | bytes 589832 | tf_op jit(solution)/shard_map/ppermute | solution.py:22
  59.8 97.9 %collective-permute-start.5 = (bf16[128,3072]{1,0:T(8,128)(2,1)}, bf16[128,3072]{1,0:T(8,128)(2,1)}, u32[]{:S(2)}, u32[]{:S(2)}) collective-permute-start(bf16[128,3072]{1,0:T(8,128)(2,1)} %fusion.1.after_ref), channel_id=1, source_target_pairs={{0,2},{1,3},{2,0},{3,1},{4,6},{5,7},{6,4},{7,5},{8,10},{9,11},{10,... | collective-permute-start | bytes 2359304 | tf_op jit(solution)/shard_map/ppermute | solution.py:284
  63.1 7.4 %collective-permute-start.2 = (bf16[128,768]{1,0:T(8,128)(2,1)S(1)}, bf16[128,768]{1,0:T(8,128)(2,1)S(1)}, u32[]{:S(2)}, u32[]{:S(2)}) collective-permute-start(bf16[128,768]{1,0:T(8,128)(2,1)S(1)} %dynamic-slice_bitcast_fusion.3), channel_id=1, source_target_pairs={{0,1},{1,0},{2,3},{3,2},{4,5},{5,4},{6,7},{7,6},{8,9},{9,8},{10,11... | collective-permute-start | bytes 589832 | tf_op jit(solution)/shard_map/ppermute | solution.py:22
  70.4 88.6 %collective-permute-start.4 = (bf16[128,3072]{1,0:T(8,128)(2,1)}, bf16[128,3072]{1,0:T(8,128)(2,1)S(1)}, u32[]{:S(2)}, u32[]{:S(2)}) collective-permute-start(bf16[128,3072]{1,0:T(8,128)(2,1)} %fusion.3), channel_id=1, source_target_pairs={{0,2},{1,3},{2,0},{3,1},{4,6},{5,7},{6,4},{7,5},{8,10},{9,11},{10,... | collective-permute-start | bytes 2359304 | tf_op jit(solution)/shard_map/ppermute | solution.py:284
  93.1 3.4 %copy-start.1 = (bf16[512,768]{1,0:T(8,128)(2,1)S(1)}, bf16[512,768]{1,0:T(8,128)(2,1)}, u32[]{:S(2)}) copy-start(bf16[512,768]{1,0:T(8,128)(2,1)} %shard_map.97) | copy-start | bytes 2359300
  93.1 10.5 %slice-start = ((s8[9437184]{0:T(1024)(128)(4,1)}), s8[4194304]{0:T(1024)(128)(4,1)S(1)}, s32[]{:S(2)}) async-start(s8[9437184]{0:T(1024)(128)(4,1)} %bitcast.54), calls=%async_computation | async-start | bytes 8388608
  93.1 10.5 %slice-start.1 = ((s8[9437184]{0:T(1024)(128)(4,1)}), s8[4194304]{0:T(1024)(128)(4,1)S(1)}, s32[]{:S(2)}) async-start(s8[9437184]{0:T(1024)(128)(4,1)} %bitcast.54), calls=%async_computation.1 | async-start | bytes 8388608
  96.5 7.1 %slice-start.2 = ((s8[9437184]{0:T(1024)(128)(4,1)}), s8[1048576]{0:T(1024)(128)(4,1)S(1)}, s32[]{:S(2)}) async-start(s8[9437184]{0:T(1024)(128)(4,1)} %bitcast.54), calls=%async_computation.2 | async-start | bytes 2097152
  103.6 1.1 copy-start.2
  104.8 54.5 %collective-permute-start.7 = (bf16[128,3072]{1,0:T(8,128)(2,1)S(1)}, bf16[128,3072]{1,0:T(8,128)(2,1)S(1)}, u32[]{:S(2)}, u32[]{:S(2)}) collective-permute-start(bf16[128,3072]{1,0:T(8,128)(2,1)S(1)} %copy-done.2), channel_id=1, source_target_pairs={{0,2},{1,3},{2,0},{3,1},{4,6},{5,7},{6,4},{7,5},{8,10},{9,11},{10,... | collective-permute-start | bytes 2359304 | tf_op jit(solution)/shard_map/ppermute | solution.py:284
  113.5 3.8 %collective-permute-start.11 = (bf16[32,768]{1,0:T(8,128)(2,1)S(1)}, bf16[32,768]{1,0:T(8,128)(2,1)S(1)}, u32[]{:S(2)}, u32[]{:S(2)}) collective-permute-start(bf16[32,768]{1,0:T(8,128)(2,1)S(1)} %get-tuple-element.5), channel_id=1, source_target_pairs={{0,1},{1,0},{2,3},{3,2},{4,5},{5,4},{6,7},{7,6},{8,9},{9,8},{10,11... | collective-permute-start | bytes 147464 | tf_op jit(solution)/shard_map/ppermute | solution.py:22
  116.9 7.6 %collective-permute-start.12 = (bf16[32,768]{1,0:T(8,128)(2,1)S(1)}, bf16[32,768]{1,0:T(8,128)(2,1)S(1)}, u32[]{:S(2)}, u32[]{:S(2)}) collective-permute-start(bf16[32,768]{1,0:T(8,128)(2,1)S(1)} %get-tuple-element.4), channel_id=1, source_target_pairs={{0,1},{1,0},{2,3},{3,2},{4,5},{5,4},{6,7},{7,6},{8,9},{9,8},{10,11... | collective-permute-start | bytes 147464 | tf_op jit(solution)/shard_map/ppermute | solution.py:22
  117.3 42.1 %collective-permute-start.6 = (bf16[128,3072]{1,0:T(8,128)(2,1)S(1)}, bf16[128,3072]{1,0:T(8,128)(2,1)S(1)}, u32[]{:S(2)}, u32[]{:S(2)}) collective-permute-start(bf16[128,3072]{1,0:T(8,128)(2,1)S(1)} %fusion.4), channel_id=1, source_target_pairs={{0,2},{1,3},{2,0},{3,1},{4,6},{5,7},{6,4},{7,5},{8,10},{9,11},{10,... | collective-permute-start | bytes 2359304 | tf_op jit(solution)/shard_map/ppermute | solution.py:284
  124.6 7.4 %collective-permute-start.3 = (bf16[256,768]{1,0:T(8,128)(2,1)S(1)}, bf16[256,768]{1,0:T(8,128)(2,1)S(1)}, u32[]{:S(2)}, u32[]{:S(2)}) collective-permute-start(bf16[256,768]{1,0:T(8,128)(2,1)S(1)} %dynamic-slice_bitcast_fusion), channel_id=1, source_target_pairs={{0,1},{1,0},{2,3},{3,2},{4,5},{5,4},{6,7},{7,6},{8,9},{9,8},{10,11... | collective-permute-start | bytes 1179656 | tf_op jit(solution)/shard_map/ppermute | solution.py:22
  132.0 24.9 %collective-permute-start.13 = (bf16[32,6144]{1,0:T(8,128)(2,1)S(1)}, bf16[32,6144]{1,0:T(8,128)(2,1)S(1)}, u32[]{:S(2)}, u32[]{:S(2)}) collective-permute-start(bf16[32,6144]{1,0:T(8,128)(2,1)S(1)} %fusion), channel_id=1, source_target_pairs={{0,2},{1,3},{2,0},{3,1},{4,6},{5,7},{6,4},{7,5},{8,10},{9,11},{10,... | collective-permute-start | bytes 1179656 | tf_op jit(solution)/shard_map/ppermute | solution.py:284
where the time goes:
time: 176 us; the launch traced here: 174 us
  matrix products  66.7 us (38%)
  Pallas kernels  53.4 us (30%)
  other arithmetic  18.6 us (11%)
  starting transfers between devices  14.5 us (8%)
  waiting for transfers between devices  9.96 us (6%)
  local copies, waits for them, and re-layouts  6.83 us (4%)
  between operations  3.63 us (2%)
    pallas_call x3, Pallas kernels, attend(): pl.pallas_call(functools.partial(attend_kernel, slot_of, given), out_shap...  48.5 us
    dot_general x10, matrix products, product(): jnp.dot(theirs, sibling_weight[:, at], preferred_element_type=jnp.float32)  39.4 us
    dot_general x10, matrix products, product(): total = jnp.dot(ours, out_weight[:, at], preferred_element_type=jnp.float32)  27.4 us
    concatenate x1, other arithmetic, local(): own_out = jnp.concatenate(done, axis=0)  14 us
    ppermute x5, starting transfers between devices, onward(): return lax.ppermute(part, 'tensor', ring)  12.8 us
    ppermute x5, waiting for transfers between devices, onward(): return lax.ppermute(part, 'tensor', ring)  9.92 us
    pallas_call x1, Pallas kernels, reach_bias(): pl.pallas_call(reach_kernel, out_shape=jax.ShapeDtypeStruct((requests, no...  4.92 us
  transfers between devices with their start and end apart: 14, of which 1 were waited for; matrix products, arithmetic and copies ran while one was open for 41% of the time, Pallas kernels for 20%

commit v1 on v0

--- a/solution.py
+++ b/solution.py
@@ -15,7 +15,7 @@
 LOW = -1e30
 CHUNK = 512
 TILES = 3
-PIECES = 2
+COLUMNS = 512
 
 
 def swapped(array, axis, bit):
@@ -234,6 +234,49 @@
     )(*scalars, queries, draft, cache, bias, after)
 
 
+def project_kernel(starts, splits, *refs):
+    ours_ref, theirs_ref, weight_ref, sibling_ref = refs[:4]
+    part_refs = refs[4 : 4 + len(starts)]
+    out_refs = refs[4 + len(starts) : 4 + len(starts) + len(splits)]
+    total_ref = refs[-1]
+    total_ref[...] = jnp.dot(
+        ours_ref[...], weight_ref[...], preferred_element_type=jnp.float32
+    ) + jnp.dot(theirs_ref[...], sibling_ref[...], preferred_element_type=jnp.float32)
+    for start, part_ref in zip(starts, part_refs):
+        total_ref[start : start + part_ref.shape[0], :] += part_ref[...].astype(jnp.float32)
+    start = 0
+    for count, out_ref in zip(splits, out_refs):
+        out_ref[...] = total_ref[start : start + count, :].astype(out_ref.dtype)
+        start += count
+
+
+def project(rows, weight, sibling, parts, splits):
+    ours, theirs = rows
+    count, depth = ours.shape
+    columns = weight.shape[1]
+    tile = math.gcd(columns, COLUMNS)
+
+    def band(size):
+        return pl.BlockSpec((size, tile), lambda s: (0, s))
+
+    whole = pl.BlockSpec((count, depth), lambda s: (0, 0))
+    return pl.pallas_call(
+        functools.partial(project_kernel, tuple(start for start, _ in parts), splits),
+        out_shape=[jax.ShapeDtypeStruct((size, columns), ours.dtype) for size in splits],
+        grid=(columns // tile,),
+        in_specs=[whole, whole, band(depth), band(depth)]
+        + [band(part.shape[0]) for _, part in parts],
+        out_specs=[band(size) for size in splits],
+        scratch_shapes=[pltpu.VMEM((count, tile), jnp.float32)],
+        cost_estimate=pl.CostEstimate(
+            flops=4 * count * depth * columns,
+            bytes_accessed=4 * depth * columns + 4 * count * columns,
+            transcendentals=0,
+        ),
+        name="project",
+    )(ours, theirs, weight, sibling, *(part for _, part in parts))
+
+
 def local(
     queries, draft_key_value, cache_kv, out_weight, tree_sizes, parents, cache_lens, block_moves
 ):
@@ -270,28 +313,20 @@
         split = 2 * count * BLK
         return cores_share(rows[:split].reshape(2, count * BLK, width)), rows[split:]
 
-    def product(rows, piece, pieces):
-        columns = out_weight.shape[1] // pieces
-        at = slice(piece * columns, (piece + 1) * columns)
-        ours, theirs = rows
-        total = jnp.dot(ours, out_weight[:, at], preferred_element_type=jnp.float32)
-        return total + jnp.dot(theirs, sibling_weight[:, at], preferred_element_type=jnp.float32)
-
     def onward(part, hop):
         ring = [
             (2 * h + l, 2 * ((h + hop) % pairs) + l) for h in range(pairs) for l in range(2)
         ]
         return lax.ppermute(part, "tensor", ring)
 
-    coming = {}
+    coming = [[] for _ in range(per_core)]
     after = bias
     for hop in range(1, pairs):
         for sub in range(per_core):
             giving = int((hop, sub) == (1, per_core - 1))
             rows, given = kept_rows(hop, sub, 1, giving, after)
-            for piece in range(PIECES):
-                part = product(rows, piece, PIECES).astype(jnp.bfloat16)
-                coming.setdefault((sub, piece), []).append(onward(part, hop))
+            (part,) = project(rows, out_weight, sibling_weight, (), (BLK,))
+            coming[sub].append(onward(part, hop))
             after = part
             if giving:
                 target = block_moves[:, 0]
@@ -310,25 +345,18 @@
         part = lax.dynamic_index_in_dim(arrived, (high + hop) % pairs, 0, keepdims=False)
         return cores_share(part)
 
-    new_coming = [
-        onward(product(new_rows(hop), 0, 1).astype(jnp.bfloat16), hop)
-        for hop in range(1, pairs)
-    ]
-
-    def total_of(rows, piece, pieces, parts):
-        total = lax.optimization_barrier(product(rows, piece, pieces))
-        for part in parts:
-            total = total + part.astype(jnp.float32)
-        return total.astype(jnp.bfloat16)
-
-    done = []
-    for sub in range(per_core):
-        rows = tuple(one[sub * BLK : (sub + 1) * BLK] for one in ours)
-        pieces = [total_of(rows, piece, PIECES, coming[sub, piece]) for piece in range(PIECES)]
-        done.append(jnp.concatenate(pieces, axis=1))
-    own_out = jnp.concatenate(done, axis=0)
-    moved_out = total_of(new_rows(0), 0, 1, new_coming)
-    return own_out, moved_out
+    new_coming = []
+    for hop in range(1, pairs):
+        rows = new_rows(hop)
+        (part,) = project(rows, out_weight, sibling_weight, (), (rows[0].shape[0],))
+        new_coming.append(onward(part, hop))
+    rows = [jnp.concatenate(two, axis=0) for two in zip(ours, new_rows(0))]
+    parts = [(sub * BLK, part) for sub in range(per_core) for part in coming[sub]]
+    share = per_core * BLK
+    parts += [(share, part) for part in new_coming]
+    return project(
+        rows, out_weight, sibling_weight, parts, (share, rows[0].shape[0] - share)
+    )
 
 
 def solution(mesh):

time: 176 us -> 158 us (0.90)
  matrix products: 66.7 us -> 0 us
  Pallas kernels: 53.4 us -> 107 us
  other arithmetic: 18.6 us -> 5.37 us
  local copies, waits for them, and re-layouts: 6.83 us -> 13.7 us
  waiting for transfers between devices: 9.96 us -> 14.6 us
  starting transfers between devices: 14.5 us -> 12.1 us
    dot_general x20 -> x0, matrix products: 66.7 us -> none  [the longest x10 39.4 us: product(): jnp.dot(theirs, sibling_weight[:, at], preferred_element_type=jnp.float32)]
    pallas_call x0 -> x4, Pallas kernels: none -> 53.6 us  [project(): pl.pallas_call(functools.partial(project_kernel, tuple((start for start,...]
    concatenate x1 -> x2, other arithmetic: 14 us -> 3.39 us  [local(): rows = [jnp.concatenate(two, axis=0) for two in zip(ours, new_rows(0))]]
    squeeze x4, local copies, waits for them, and re-layouts: 1.78 us -> 5.03 us  [cores_share(): theirs = lax.dynamic_index_in_dim(rows, 1 - low, 0, keepdims=False)]
    ppermute x9, waiting for transfers between devices: 0.04 us -> 3.18 us  [swapped(): lax.ppermute(array, axis, [(i, i ^ bit) for i in range(lax.axis_size(axis...]
    unnamed x15 -> x13, local copies, waits for them, and re-layouts: 1.7 us -> 4.64 us
    convert_element_type x5 -> x0, other arithmetic: 2.64 us -> none  [total_of(): return total.astype(jnp.bfloat16)]
    ppermute x5 -> x3, starting transfers between devices: 12.8 us -> 10.7 us  [onward(): return lax.ppermute(part, 'tensor', ring)]
  transfers between devices with their start and end apart: 14 -> 12, of which waited for: 1 -> 4; matrix products, arithmetic and copies ran while one was open for 41% -> 9% of each run, Pallas kernels for 20% -> 39%
where the time goes in v1:
time: 158 us; the launch traced here: 156 us
  Pallas kernels  107 us (68%)
  waiting for transfers between devices  14.6 us (9%)
  local copies, waits for them, and re-layouts  13.7 us (9%)
  starting transfers between devices  12.1 us (8%)
  other arithmetic  5.37 us (3%)
  between operations  3.34 us (2%)
    pallas_call x4, Pallas kernels, project(): pl.pallas_call(functools.partial(project_kernel, tuple((start for start,...  53.6 us
    pallas_call x3, Pallas kernels, attend(): pl.pallas_call(functools.partial(attend_kernel, slot_of, given), out_shap...  48.4 us
    ppermute x3, waiting for transfers between devices, onward(): return lax.ppermute(part, 'tensor', ring)  11.4 us
    ppermute x3, starting transfers between devices, onward(): return lax.ppermute(part, 'tensor', ring)  10.7 us
    squeeze x4, local copies, waits for them, and re-layouts, cores_share(): theirs = lax.dynamic_index_in_dim(rows, 1 - low, 0, keepdims=False)  5.03 us
    pallas_call x1, Pallas kernels, reach_bias(): pl.pallas_call(reach_kernel, out_shape=jax.ShapeDtypeStruct((requests, no...  4.92 us
    unnamed x13, local copies, waits for them, and re-layouts  4.64 us
    concatenate x2, other arithmetic, local(): rows = [jnp.concatenate(two, axis=0) for two in zip(ours, new_rows(0))]  3.39 us
  transfers between devices with their start and end apart: 12, of which 4 were waited for; matrix products, arithmetic and copies ran while one was open for 9% of the time, Pallas kernels for 39%

profile of v1, /device:TPU:22, one launch (start us, length us, event | category | flops | bytes accessed | tf_op | source)
XLA Modules:
  0.0 156.1 jit_solution(13667122430987838907)
XLA Ops:
  0.6 0.1 collective-permute-start.1
  0.7 1.3 copy.12.moves_ref
  2.1 1.4 reshape.27.parent_ref
  3.5 0.7 pad_add_fusion.ids_ref
  4.1 4.9 %reach.1.bias_ref.after_ref = f32[2,512,512]{2,1,0:T(8,128)} custom-call(s32[3]{0:T(128)} %pad_add_fusion.ids_ref, s32[8,2,512]{2,1,0:T(2,128)} %reshape.27.parent_ref), custom_call_target="tpu_custom_call" | custom-call | flops 1000000000 | bytes 2097152 | tf_op jit(solution)/shard_map/reach/pallas_call | solution.py:66
  9.0 13.8 %shard_map.95 = bf16[256,768]{1,0:T(8,128)(2,1)} custom-call(s32[3]{0:T(128)} %pad_add_fusion.ids_ref, s32[16]{0:T(128)} %sizes_ref.5, s32[16]{0:T(128)} %lengths_ref.5, s32[8,2]{1,0:T(8,128)} %copy.12.moves_ref, bf16[2,512,768]{2,1,0:T(8,128)(2,1)} %q_ref.5, bf16[2,2,512,128]{3,2,1,0:T(8,128)(2,1)} %draft_ref.5, bf16[2,2,1792,128]{3,2,1,0:T(8,128)(2,1)} %cache_ref.5, ...), custom_call_target="tpu_custom_call" | custom-call | flops 1811939328 | bytes 3145728 | tf_op jit(solution)/shard_map/pallas_call | solution.py:225
  22.9 1.7 %dynamic-slice_bitcast_fusion.4 = (bf16[128,768]{1,0:T(8,128)(2,1)S(1)}, bf16[128,768]{1,0:T(8,128)(2,1)}) fusion(bf16[2,128,768]{2,1,0:T(8,128)(2,1)} %bitcast.30, s32[]{:T(128)S(6)} %select_n.78, s32[]{:T(128)S(6)} %select_n.77), kind=kLoop, calls=%fused_computation.7 | loop fusion | bytes 786440 | tf_op jit(solution)/shard_map/jit(dynamic_index_in_dim)/squeeze | solution.py:300
  24.6 0.5 collective-permute-start
  25.0 1.1 collective-permute-done.refs_1_
  26.1 0.0 copy-start.4
  26.1 0.0 collective-permute-done.1.refs_3_
  26.1 0.7 copy-done.4
  26.8 12.8 %project.4.after_ref = bf16[128,6144]{1,0:T(8,128)(2,1)} custom-call(bf16[128,768]{1,0:T(8,128)(2,1)} %get-tuple-element.9.refs_0_, bf16[128,768]{1,0:T(8,128)(2,1)} %copy-done.4, bf16[768,6144]{1,0:T(8,128)(2,1)} %refs_2_.7, bf16[768,6144]{1,0:T(8,128)(2,1)} %collective-permute-done.1.refs_3_), custom_call_target="tpu_custom_call" | custom-call | flops 2415919104 | bytes 22020096 | tf_op jit(solution)/shard_map/project/pallas_call | solution.py:263
  39.6 0.0 copy-start
  39.6 18.3 %shard_map.96 = bf16[384,768]{1,0:T(8,128)(2,1)} custom-call(s32[3]{0:T(128)} %pad_add_fusion.ids_ref, s32[16]{0:T(128)} %sizes_ref.5, s32[16]{0:T(128)} %lengths_ref.5, s32[8,2]{1,0:T(8,128)} %copy.12.moves_ref, bf16[2,512,768]{2,1,0:T(8,128)(2,1)} %q_ref.5, bf16[2,2,512,128]{3,2,1,0:T(8,128)(2,1)} %draft_ref.5, bf16[2,2,1792,128]{3,2,1,0:T(8,128)(2,1)} %cache_ref.5, ...), custom_call_target="tpu_custom_call" | custom-call | flops 2717908992 | bytes 3538944 | tf_op jit(solution)/shard_map/pallas_call | solution.py:225
  57.9 1.0 slice.12
  58.9 0.7 dynamic-slice_bitcast_fusion.2
  59.6 0.4 collective-permute-start.2
  60.0 0.0 copy-done
  60.0 0.0 collective-permute-start.8
  60.0 1.1 collective-permute-done.2.refs_1_
  61.1 0.0 copy-start.3
  61.1 0.7 copy-done.3
  61.8 0.0 copy-start.5
  61.8 12.8 %project.5.after_ref = bf16[128,6144]{1,0:T(8,128)(2,1)} custom-call(bf16[128,768]{1,0:T(8,128)(2,1)} %get-tuple-element.7.refs_0_, bf16[128,768]{1,0:T(8,128)(2,1)} %copy-done.3, bf16[768,6144]{1,0:T(8,128)(2,1)} %refs_2_.7, bf16[768,6144]{1,0:T(8,128)(2,1)} %collective-permute-done.1.refs_3_), custom_call_target="tpu_custom_call" | custom-call | flops 2415919104 | bytes 22020096 | tf_op jit(solution)/shard_map/project/pallas_call | solution.py:263
  74.6 0.9 collective-permute-start.9
  75.5 0.0 copy-done.5
  75.5 0.6 select_reduce_fusion
  76.8 0.6 reduce_or.9
  79.4 1.6 %slice.13 = bf16[128,768]{1,0:T(8,128)(2,1)} slice(bf16[384,768]{1,0:T(8,128)(2,1)} %shard_map.96), slice={[256:384], [0:768]} | slice | bytes 393216 | tf_op jit(solution)/shard_map/slice | solution.py:314
  81.0 0.0 collective-permute-start.5
  81.0 0.0 collective-permute-start.4
  81.0 0.0 collective-permute-start.3
  81.1 16.3 %shard_map.97 = bf16[512,768]{1,0:T(8,128)(2,1)} custom-call(s32[3]{0:T(128)} %pad_add_fusion.ids_ref, s32[16]{0:T(128)} %sizes_ref.5, s32[16]{0:T(128)} %lengths_ref.5, s32[8,2]{1,0:T(8,128)} %copy.12.moves_ref, bf16[2,512,768]{2,1,0:T(8,128)(2,1)} %q_ref.5, bf16[2,2,512,128]{3,2,1,0:T(8,128)(2,1)} %draft_ref.5, bf16[2,2,1792,128]{3,2,1,0:T(8,128)(2,1)} %cache_ref.5, ...), custom_call_target="tpu_custom_call" | custom-call | flops 3623878656 | bytes 3932160 | tf_op jit(solution)/shard_map/pallas_call | solution.py:225
  97.4 1.9 %dynamic-slice_bitcast_fusion = (bf16[256,768]{1,0:T(8,128)(2,1)}, bf16[256,768]{1,0:T(8,128)(2,1)S(1)}) fusion(bf16[2,256,768]{2,1,0:T(8,128)(2,1)} %bitcast.33, s32[]{:T(128)S(6)} %select_n.78, s32[]{:T(128)S(6)} %select_n.77), kind=kLoop, calls=%fused_computation.2 | loop fusion | bytes 1572872 | tf_op jit(solution)/shard_map/jit(dynamic_index_in_dim)/squeeze | solution.py:300
  99.3 0.0 collective-permute-done.5
  99.3 0.0 collective-permute-start.6
  99.3 0.0 collective-permute-done.4
  99.3 0.0 collective-permute-done.3
  99.3 0.1 select_select_fusion
  99.4 0.7 dynamic-slice_bitcast_fusion.6
  100.1 0.5 collective-permute-start.10
  100.6 1.0 collective-permute-done.10.refs_1_
  101.6 12.4 %project.6 = bf16[32,6144]{1,0:T(8,128)(2,1)} custom-call(bf16[32,768]{1,0:T(8,128)(2,1)} %get-tuple-element.11.refs_0_, bf16[32,768]{1,0:T(8,128)(2,1)} %collective-permute-done.10.refs_1_, bf16[768,6144]{1,0:T(8,128)(2,1)} %refs_2_.7, bf16[768,6144]{1,0:T(8,128)(2,1)} %collective-permute-done.1.refs_3_), custom_call_target="tpu_custom_call" | custom-call | flops 603979776 | bytes 19660800 | tf_op jit(solution)/shard_map/project/pallas_call | solution.py:263
  114.0 9.7 %collective-permute-start.11 = (bf16[32,6144]{1,0:T(8,128)(2,1)}, bf16[32,6144]{1,0:T(8,128)(2,1)S(1)}, u32[]{:S(2)}, u32[]{:S(2)}) collective-permute-start(bf16[32,6144]{1,0:T(8,128)(2,1)} %project.6), channel_id=1, source_target_pairs={{0,2},{1,3},{2,0},{3,1},{4,6},{5,7},{6,4},{7,5},{8,10},{9,11},{10,... | collective-permute-start | bytes 1179656 | tf_op jit(solution)/shard_map/ppermute | solution.py:320
  123.7 0.1 collective-permute-start.7
  123.7 1.6 %pad_maximum_fusion.refs_0_ = bf16[288,768]{1,0:T(8,128)(2,1)} fusion(bf16[32,768]{1,0:T(8,128)(2,1)} %get-tuple-element.13, bf16[256,768]{1,0:T(8,128)(2,1)S(1)} %get-tuple-element.5), kind=kLoop, calls=%fused_computation | loop fusion | flops 884736 | bytes 884736 | tf_op jit(solution)/shard_map/concatenate | solution.py:353
  125.3 0.0 collective-permute-done.7
  125.3 0.0 collective-permute-done.6
  125.3 1.8 %pad_maximum_fusion.1.refs_1_ = bf16[288,768]{1,0:T(8,128)(2,1)} fusion(bf16[32,768]{1,0:T(8,128)(2,1)S(1)} %collective-permute-done.7, bf16[256,768]{1,0:T(8,128)(2,1)} %collective-permute-done.6), kind=kLoop, calls=%fused_computation.1 | loop fusion | flops 884736 | bytes 884736 | tf_op jit(solution)/shard_map/concatenate | solution.py:353
  127.1 11.4 %collective-permute-done.11.refs_6_ = bf16[32,6144]{1,0:T(8,128)(2,1)S(1)} collective-permute-done((bf16[32,6144]{1,0:T(8,128)(2,1)}, bf16[32,6144]{1,0:T(8,128)(2,1)S(1)}, u32[]{:S(2)}, u32[]{:S(2)}) %collective-permute-start.11) | collective-permute-done | bytes 393248 | tf_op jit(solution)/shard_map/ppermute | solution.py:320
  138.6 0.0 copy-start.2
  138.6 0.0 collective-permute-done.8.refs_4_
  138.6 0.8 copy-done.2
  139.3 0.0 copy-start.1
  139.3 0.0 collective-permute-done.9.refs_5_
  139.3 1.2 copy-done.1
  140.5 15.6 %project.7 = (bf16[256,6144]{1,0:T(8,128)(2,1)}, bf16[32,6144]{1,0:T(8,128)(2,1)}) custom-call(bf16[288,768]{1,0:T(8,128)(2,1)} %pad_maximum_fusion.refs_0_, bf16[288,768]{1,0:T(8,128)(2,1)} %pad_maximum_fusion.1.refs_1_, bf16[768,6144]{1,0:T(8,128)(2,1)} %refs_2_.7, bf16[768,6144]{1,0:T(8,128)(2,1)} %collective-permute-done.1.refs_3_, ...), custom_call_target="tpu_custom_call" | custom-call | flops 5435817984 | bytes 25952256 | tf_op jit(solution)/shard_map/project/pallas_call | solution.py:263
Async XLA Ops:
  0.6 25.5 %collective-permute-start.1 = (bf16[768,6144]{1,0:T(8,128)(2,1)}, bf16[768,6144]{1,0:T(8,128)(2,1)}, u32[]{:S(2)}, u32[]{:S(2)}) collective-permute-start(bf16[768,6144]{1,0:T(8,128)(2,1)} %refs_2_.7), channel_id=1, source_target_pairs={{0,1},{1,0},{2,3},{3,2},{4,5},{5,4},{6,7},{7,6},{8,9},{9,8},{10,11... | collective-permute-start | bytes 28311560 | tf_op jit(solution)/shard_map/ppermute | solution.py:22
  24.6 1.5 collective-permute-start
  26.1 0.7 copy-start.4
  39.6 20.4 %copy-start = (bf16[128,6144]{1,0:T(8,128)(2,1)S(1)}, bf16[128,6144]{1,0:T(8,128)(2,1)}, u32[]{:S(2)}) copy-start(bf16[128,6144]{1,0:T(8,128)(2,1)} %project.4.after_ref) | copy-start | bytes 4718596
  59.6 1.4 collective-permute-start.2
  60.0 78.6 %collective-permute-start.8 = (bf16[128,6144]{1,0:T(8,128)(2,1)S(1)}, bf16[128,6144]{1,0:T(8,128)(2,1)S(1)}, u32[]{:S(2)}, u32[]{:S(2)}) collective-permute-start(bf16[128,6144]{1,0:T(8,128)(2,1)S(1)} %copy-done), channel_id=1, source_target_pairs={{0,2},{1,3},{2,0},{3,1},{4,6},{5,7},{6,4},{7,5},{8,10},{9,11},{10,... | collective-permute-start | bytes 4718600 | tf_op jit(solution)/shard_map/ppermute | solution.py:320
  61.1 0.7 copy-start.3
  61.8 13.8 %copy-start.5 = (s32[8,2]{0,1:T(2,128)S(1)}, s32[8,2]{0,1:T(2,128)}, u32[]{:S(2)}) copy-start(s32[8,2]{0,1:T(2,128)} %param.15) | copy-start | bytes 196
  74.6 64.7 %collective-permute-start.9 = (bf16[128,6144]{1,0:T(8,128)(2,1)}, bf16[128,6144]{1,0:T(8,128)(2,1)}, u32[]{:S(2)}, u32[]{:S(2)}) collective-permute-start(bf16[128,6144]{1,0:T(8,128)(2,1)} %project.5.after_ref), channel_id=1, source_target_pairs={{0,2},{1,3},{2,0},{3,1},{4,6},{5,7},{6,4},{7,5},{8,10},{9,11},{10,... | collective-permute-start | bytes 4718600 | tf_op jit(solution)/shard_map/ppermute | solution.py:320
  81.0 18.3 %collective-permute-start.5 = (bf16[128,768]{1,0:T(8,128)(2,1)}, bf16[128,768]{1,0:T(8,128)(2,1)}, u32[]{:S(2)}, u32[]{:S(2)}) collective-permute-start(bf16[128,768]{1,0:T(8,128)(2,1)} %slice.13), channel_id=1, source_target_pairs={{0,4},{4,0},{8,12},{12,8},{16,20},{20,16},{24,28},{28,24},{1,5},{5... | collective-permute-start | bytes 589832 | tf_op jit(solution)/shard_map/ppermute | solution.py:22
  81.0 18.3 %collective-permute-start.4 = (bf16[128,768]{1,0:T(8,128)(2,1)}, bf16[128,768]{1,0:T(8,128)(2,1)}, u32[]{:S(2)}, u32[]{:S(2)}) collective-permute-start(bf16[128,768]{1,0:T(8,128)(2,1)} %slice.13), channel_id=1, source_target_pairs={{0,8},{4,12},{8,0},{12,4},{16,24},{20,28},{24,16},{28,20},{1,9},{5... | collective-permute-start | bytes 589832 | tf_op jit(solution)/shard_map/ppermute | solution.py:22
  81.0 18.3 %collective-permute-start.3 = (bf16[128,768]{1,0:T(8,128)(2,1)}, bf16[128,768]{1,0:T(8,128)(2,1)}, u32[]{:S(2)}, u32[]{:S(2)}) collective-permute-start(bf16[128,768]{1,0:T(8,128)(2,1)} %slice.13), channel_id=1, source_target_pairs={{0,16},{4,20},{8,24},{12,28},{16,0},{20,4},{24,8},{28,12},{1,17},{... | collective-permute-start | bytes 589832 | tf_op jit(solution)/shard_map/ppermute | solution.py:22
  99.3 26.0 %collective-permute-start.6 = (bf16[256,768]{1,0:T(8,128)(2,1)}, bf16[256,768]{1,0:T(8,128)(2,1)}, u32[]{:S(2)}, u32[]{:S(2)}) collective-permute-start(bf16[256,768]{1,0:T(8,128)(2,1)} %get-tuple-element.4), channel_id=1, source_target_pairs={{0,1},{1,0},{2,3},{3,2},{4,5},{5,4},{6,7},{7,6},{8,9},{9,8},{10,11... | collective-permute-start | bytes 1179656 | tf_op jit(solution)/shard_map/ppermute | solution.py:22
  100.1 1.5 collective-permute-start.10
  114.0 24.6 %collective-permute-start.11 = (bf16[32,6144]{1,0:T(8,128)(2,1)}, bf16[32,6144]{1,0:T(8,128)(2,1)S(1)}, u32[]{:S(2)}, u32[]{:S(2)}) collective-permute-start(bf16[32,6144]{1,0:T(8,128)(2,1)} %project.6), channel_id=1, source_target_pairs={{0,2},{1,3},{2,0},{3,1},{4,6},{5,7},{6,4},{7,5},{8,10},{9,11},{10,... | collective-permute-start | bytes 1179656 | tf_op jit(solution)/shard_map/ppermute | solution.py:320
  123.7 1.7 %collective-permute-start.7 = (bf16[32,768]{1,0:T(8,128)(2,1)}, bf16[32,768]{1,0:T(8,128)(2,1)S(1)}, u32[]{:S(2)}, u32[]{:S(2)}) collective-permute-start(bf16[32,768]{1,0:T(8,128)(2,1)} %get-tuple-element.12), channel_id=1, source_target_pairs={{0,1},{1,0},{2,3},{3,2},{4,5},{5,4},{6,7},{7,6},{8,9},{9,8},{10,11... | collective-permute-start | bytes 147464 | tf_op jit(solution)/shard_map/ppermute | solution.py:22
  138.6 0.8 copy-start.2
  139.3 1.2 copy-start.1
